TPU v7x, 512 devices: a whole 4x4x16 slice. The times are simulated.
512 devices in a mesh: vir: 64 (over z, x_lo, core), occ: 8 (over y, x_hi).
Axes of the slice: x: 4 (x_hi: 2, x_lo: 2; x = x_hi * 2 + x_lo), y: 4, z: 16, core: 2. Of those that a mesh axis runs over, the one named last changes fastest.
Arguments:
- tau_amps: bfloat16 [4096, 32768], P('occ', 'vir'), may hold values from -6 to 6
- lambda_amps: bfloat16 [4096, 32768], P('occ', 'vir'), may hold values from -0.09375 to 0.09375
Outputs:
- density: float32 [32768, 5, 512], P(('vir', 'occ'))
All inputs are finite; a program needn't handle non-finite values.
Results may differ from a plain program's by a relative error of at most 0.01.
Values may be sent and summed in bfloat16 or wider, within the bound.
A program may use at most 64 MiB of HBM per device.

v0:
```python
import jax
import jax.numpy as jnp
from jax import lax
from jax.sharding import PartitionSpec as P

REACH = 4


def from_behind(array, axis, by):
    count = lax.axis_size(axis)
    return lax.ppermute(array, axis, [(i, (i + by) % count) for i in range(count)])


def in_blocks(array, dim, count):
    before, after = (array.shape[:dim], array.shape[dim + 1 :])
    return jnp.moveaxis(array.reshape(*before, count, -1, *after), dim, 0)


def sent_and_summed(array, axis, dim):
    count = lax.axis_size(axis)
    pieces = lax.all_to_all(in_blocks(array, dim, count), axis, 0, 0, tiled=True)
    return jnp.sum(pieces.astype(jnp.float32), axis=0)


def pair_block(tau_amps, lambda_amps, remote):
    contract = (((0,), (0,)), ((), ()))
    left_half = lax.dot_general(tau_amps, remote[1], contract, preferred_element_type=jnp.float32)
    right_half = lax.dot_general(
        lambda_amps, remote[0], contract, preferred_element_type=jnp.float32
    )
    return 0.5 * (left_half + right_half)


def on_device(tau_amps, lambda_amps):
    stacked = jnp.stack((tau_amps, lambda_amps), 0)
    partials = [pair_block(tau_amps, lambda_amps, stacked)]
    remote = stacked
    for offset in range(1, REACH + 1):
        remote = from_behind(remote, "vir", -1)
        partials.append(pair_block(tau_amps, lambda_amps, remote))
    return sent_and_summed(jnp.stack(partials, 1).astype(jnp.bfloat16), "occ", 0)


def solution(mesh):
    placed = (P("occ", "vir"), P("occ", "vir"))
    return jax.shard_map(
        on_device,
        mesh=mesh,
        in_specs=placed,
        out_specs=P(("vir", "occ"), None, None),
        check_vma=False,
    )
```

profile of v0, /device:TPU:8, one launch (start us, length us, event | category | flops | bytes accessed | tf_op | source)
XLA Modules:
  0.0 115.8 jit_solution(8302651699194551550)
XLA Ops:
  0.0 1.4 %pad_maximum_fusion = bf16[2,512,512]{2,1,0:T(8,128)(2,1)S(1)} fusion(bf16[1,512,512]{2,1,0:T(8,128)(2,1)} %bitcast.52, bf16[1,512,512]{2,1,0:T(8,128)(2,1)} %bitcast.51), kind=kLoop, calls=%fused_computation.20 | loop fusion | flops 524288 | bytes 2097152 | tf_op jit(solution)/shard_map/stack | solution.py:35
  1.4 11.8 %collective-permute-start = (bf16[2,512,512]{2,1,0:T(8,128)(2,1)S(1)}, bf16[2,512,512]{2,1,0:T(8,128)(2,1)S(1)}, u32[]{:S(2)}, u32[]{:S(2)}) collective-permute-start(bf16[2,512,512]{2,1,0:T(8,128)(2,1)S(1)} %pad_maximum_fusion), channel_id=1, source_target_pairs={{0,504},{8,0},{16,8},{24,16},{32,24},{40,32},{48,40},{56,48},{64,5... | collective-permute-start | bytes 3145736 | tf_op jit(solution)/shard_map/ppermute | solution.py:11
  13.2 12.3 %collective-permute-done = bf16[2,512,512]{2,1,0:T(8,128)(2,1)S(1)} collective-permute-done((bf16[2,512,512]{2,1,0:T(8,128)(2,1)S(1)}, bf16[2,512,512]{2,1,0:T(8,128)(2,1)S(1)}, u32[]{:S(2)}, u32[]{:S(2)}) %collective-permute-start) | collective-permute-done | bytes 1048608 | tf_op jit(solution)/shard_map/ppermute | solution.py:11
  25.5 5.9 %collective-permute-start.1 = (bf16[2,512,512]{2,1,0:T(8,128)(2,1)S(1)}, bf16[2,512,512]{2,1,0:T(8,128)(2,1)}, u32[]{:S(2)}, u32[]{:S(2)}) collective-permute-start(bf16[2,512,512]{2,1,0:T(8,128)(2,1)S(1)} %collective-permute-done), channel_id=1, source_target_pairs={{0,504},{8,0},{16,8},{24,16},{32,24},{40,32},{48,40},{56,48},{64,5... | collective-permute-start | bytes 3145736 | tf_op jit(solution)/shard_map/ppermute | solution.py:11
  31.4 1.7 %fusion.18 = f32[512,512]{1,0:T(8,128)S(1)} fusion(bf16[512,512]{1,0:T(8,128)(2,1)} %param.2, bf16[512,512]{1,0:T(8,128)(2,1)} %param.3), kind=kOutput, calls=%fused_computation.38 | convolution fusion | flops 268435456 | bytes 2097152 | tf_op jit(solution)/shard_map/dot_general | solution.py:27
  33.1 0.5 fusion.5
  33.5 10.1 %collective-permute-done.1 = bf16[2,512,512]{2,1,0:T(8,128)(2,1)} collective-permute-done((bf16[2,512,512]{2,1,0:T(8,128)(2,1)S(1)}, bf16[2,512,512]{2,1,0:T(8,128)(2,1)}, u32[]{:S(2)}, u32[]{:S(2)}) %collective-permute-start.1) | collective-permute-done | bytes 1048608 | tf_op jit(solution)/shard_map/ppermute | solution.py:11
  43.7 6.0 %collective-permute-start.2 = (bf16[2,512,512]{2,1,0:T(8,128)(2,1)}, bf16[2,512,512]{2,1,0:T(8,128)(2,1)S(1)}, u32[]{:S(2)}, u32[]{:S(2)}) collective-permute-start(bf16[2,512,512]{2,1,0:T(8,128)(2,1)} %collective-permute-done.1), channel_id=1, source_target_pairs={{0,504},{8,0},{16,8},{24,16},{32,24},{40,32},{48,40},{56,48},{64,5... | collective-permute-start | bytes 3145736 | tf_op jit(solution)/shard_map/ppermute | solution.py:11
  49.7 0.8 constant_dynamic-update-slice_fusion.4
  51.7 0.8 constant_dynamic-update-slice_fusion.3
  52.5 1.5 %fusion.16 = f32[512,512]{1,0:T(8,128)S(1)} fusion(bf16[512,512]{1,0:T(8,128)(2,1)S(1)} %copy-done.1, bf16[2,512,512]{2,1,0:T(8,128)(2,1)} %collective-permute-done.1), kind=kOutput, calls=%fused_computation.28 | convolution fusion | flops 268435456 | bytes 2097152 | tf_op jit(solution)/shard_map/dot_general | solution.py:28
  54.0 8.3 %collective-permute-done.2 = bf16[2,512,512]{2,1,0:T(8,128)(2,1)S(1)} collective-permute-done((bf16[2,512,512]{2,1,0:T(8,128)(2,1)}, bf16[2,512,512]{2,1,0:T(8,128)(2,1)S(1)}, u32[]{:S(2)}, u32[]{:S(2)}) %collective-permute-start.2) | collective-permute-done | bytes 1048608 | tf_op jit(solution)/shard_map/ppermute | solution.py:11
  62.3 5.8 %collective-permute-start.3 = (bf16[2,512,512]{2,1,0:T(8,128)(2,1)S(1)}, bf16[2,512,512]{2,1,0:T(8,128)(2,1)}, u32[]{:S(2)}, u32[]{:S(2)}) collective-permute-start(bf16[2,512,512]{2,1,0:T(8,128)(2,1)S(1)} %collective-permute-done.2), channel_id=1, source_target_pairs={{0,504},{8,0},{16,8},{24,16},{32,24},{40,32},{48,40},{56,48},{64,5... | collective-permute-start | bytes 3145736 | tf_op jit(solution)/shard_map/ppermute | solution.py:11
  68.1 1.5 %fusion.12 = bf16[512,512]{0,1:T(8,128)(2,1)S(1)} fusion(f32[512,512]{1,0:T(8,128)S(1)} %fusion.16, bf16[512,512]{1,0:T(8,128)(2,1)S(1)} %copy-done, bf16[2,512,512]{2,1,0:T(8,128)(2,1)} %collective-permute-done.1), kind=kOutput, calls=%fused_computation.18 | convolution fusion | flops 269221888 | bytes 2621440 | tf_op jit(solution)/shard_map/dot_general | solution.py:27
  69.9 0.9 constant_dynamic-update-slice_fusion.2
  71.2 0.5 fusion.11
  71.9 0.8 constant_dynamic-update-slice_fusion.1
  72.7 7.7 %collective-permute-done.3 = bf16[2,512,512]{2,1,0:T(8,128)(2,1)} collective-permute-done((bf16[2,512,512]{2,1,0:T(8,128)(2,1)S(1)}, bf16[2,512,512]{2,1,0:T(8,128)(2,1)}, u32[]{:S(2)}, u32[]{:S(2)}) %collective-permute-start.3) | collective-permute-done | bytes 1048608 | tf_op jit(solution)/shard_map/ppermute | solution.py:11
  80.4 1.5 %fusion.14 = f32[512,512]{1,0:T(8,128)S(1)} fusion(bf16[512,512]{1,0:T(8,128)(2,1)S(1)} %copy-done.1, bf16[2,512,512]{2,1,0:T(8,128)(2,1)} %collective-permute-done.3), kind=kOutput, calls=%fused_computation.22 | convolution fusion | flops 268435456 | bytes 2097152 | tf_op jit(solution)/shard_map/dot_general | solution.py:28
  81.9 1.5 %fusion.10 = bf16[512,512]{0,1:T(8,128)(2,1)S(1)} fusion(f32[512,512]{1,0:T(8,128)S(1)} %fusion.14, bf16[512,512]{1,0:T(8,128)(2,1)S(1)} %copy-done, bf16[2,512,512]{2,1,0:T(8,128)(2,1)} %collective-permute-done.3), kind=kOutput, calls=%fused_computation.16 | convolution fusion | flops 269221888 | bytes 2621440 | tf_op jit(solution)/shard_map/dot_general | solution.py:27
  83.7 0.8 constant_dynamic-update-slice_fusion
  84.5 1.9 %copy.39 = bf16[8,64,5,512]{3,1,2,0:T(8,128)(2,1)S(1)} copy(bf16[8,64,5,512]{3,1,0,2:T(8,128)(2,1)} %constant_dynamic-update-slice_fusion) | data formatting | bytes 5242880 | tf_op jit(solution)/shard_map/stack | solution.py:41
  86.4 28.2 %all_to_all.5 = bf16[8,64,5,512]{3,1,2,0:T(8,128)(2,1)S(1)} all-to-all(bf16[8,64,5,512]{3,1,2,0:T(8,128)(2,1)S(1)} %copy.39), channel_id=1, replica_groups=mesh['vir'=64,'occ'=8] {'occ'}, dimensions={0} | all-to-all | bytes 5242880 | tf_op jit(solution)/shard_map/all_to_all | solution.py:21
  114.6 1.2 %convert_reduce_fusion = f32[64,5,512]{2,0,1:T(8,128)} fusion(bf16[8,64,5,512]{3,1,2,0:T(8,128)(2,1)S(1)} %all_to_all.5), kind=kLoop, calls=%fused_computation | loop fusion | flops 2457600 | bytes 3276800 | tf_op jit(solution)/shard_map/reduce_sum | solution.py:22
  (11 shorter events, 2.2 us)
Async XLA Ops:
  0.0 33.1 %copy-start.1 = (bf16[512,512]{1,0:T(8,128)(2,1)S(1)}, bf16[512,512]{1,0:T(8,128)(2,1)}, u32[]{:S(2)}) copy-start(bf16[512,512]{1,0:T(8,128)(2,1)} %param.3) | copy-start | bytes 1572868
  0.0 33.1 %copy-start = (bf16[512,512]{1,0:T(8,128)(2,1)S(1)}, bf16[512,512]{1,0:T(8,128)(2,1)}, u32[]{:S(2)}) copy-start(bf16[512,512]{1,0:T(8,128)(2,1)} %param.2) | copy-start | bytes 1572868
  1.4 24.1 %collective-permute-start = (bf16[2,512,512]{2,1,0:T(8,128)(2,1)S(1)}, bf16[2,512,512]{2,1,0:T(8,128)(2,1)S(1)}, u32[]{:S(2)}, u32[]{:S(2)}) collective-permute-start(bf16[2,512,512]{2,1,0:T(8,128)(2,1)S(1)} %pad_maximum_fusion), channel_id=1, source_target_pairs={{0,504},{8,0},{16,8},{24,16},{32,24},{40,32},{48,40},{56,48},{64,5... | collective-permute-start | bytes 3145736 | tf_op jit(solution)/shard_map/ppermute | solution.py:11
  25.5 18.2 %collective-permute-start.1 = (bf16[2,512,512]{2,1,0:T(8,128)(2,1)S(1)}, bf16[2,512,512]{2,1,0:T(8,128)(2,1)}, u32[]{:S(2)}, u32[]{:S(2)}) collective-permute-start(bf16[2,512,512]{2,1,0:T(8,128)(2,1)S(1)} %collective-permute-done), channel_id=1, source_target_pairs={{0,504},{8,0},{16,8},{24,16},{32,24},{40,32},{48,40},{56,48},{64,5... | collective-permute-start | bytes 3145736 | tf_op jit(solution)/shard_map/ppermute | solution.py:11
  43.7 18.6 %collective-permute-start.2 = (bf16[2,512,512]{2,1,0:T(8,128)(2,1)}, bf16[2,512,512]{2,1,0:T(8,128)(2,1)S(1)}, u32[]{:S(2)}, u32[]{:S(2)}) collective-permute-start(bf16[2,512,512]{2,1,0:T(8,128)(2,1)} %collective-permute-done.1), channel_id=1, source_target_pairs={{0,504},{8,0},{16,8},{24,16},{32,24},{40,32},{48,40},{56,48},{64,5... | collective-permute-start | bytes 3145736 | tf_op jit(solution)/shard_map/ppermute | solution.py:11
  62.3 18.1 %collective-permute-start.3 = (bf16[2,512,512]{2,1,0:T(8,128)(2,1)S(1)}, bf16[2,512,512]{2,1,0:T(8,128)(2,1)}, u32[]{:S(2)}, u32[]{:S(2)}) collective-permute-start(bf16[2,512,512]{2,1,0:T(8,128)(2,1)S(1)} %collective-permute-done.2), channel_id=1, source_target_pairs={{0,504},{8,0},{16,8},{24,16},{32,24},{40,32},{48,40},{56,48},{64,5... | collective-permute-start | bytes 3145736 | tf_op jit(solution)/shard_map/ppermute | solution.py:11
where the time goes:
time: 116 us
  waiting for transfers between devices  38.4 us (33%)
  starting transfers between devices  29.5 us (25%)
  blocking collectives  28.2 us (24%)
  matrix products  10 us (9%)
  local copies, waits for them, and re-layouts  6.96 us (6%)
  other arithmetic  2.6 us (2%)
    ppermute x4, waiting for transfers between devices, from_behind(): lax.ppermute(array, axis, [(i, (i + by) % count) for i in range(count)])  38.4 us
    ppermute x4, starting transfers between devices, from_behind(): lax.ppermute(array, axis, [(i, (i + by) % count) for i in range(count)])  29.5 us
    all_to_all x1, blocking collectives, sent_and_summed(): lax.all_to_all(in_blocks(array, dim, count), axis, 0, 0, tiled=True)  28.2 us
    dot_general x5, matrix products, pair_block(): lax.dot_general(tau_amps, remote[1], contract, preferred_element_type=jnp...  5.62 us
    dot_general x5, matrix products, pair_block(): lax.dot_general(lambda_amps, remote[0], contract, preferred_element_type=...  4.39 us
    unnamed x8, local copies, waits for them, and re-layouts  3.37 us
    another operation x2, local copies, waits for them, and re-layouts, on_device(): jnp.stack(partials, 1).astype(jnp.bfloat16)  2.74 us
  transfers between devices with their start and end apart: 4, of which 4 were waited for; matrix products, arithmetic and copies ran while one was open for 9% of the time, Pallas kernels for 0%

commit v1 on v0

v1 whole, which is shorter than its diff:
```python
import jax
import jax.numpy as jnp
from jax import lax
from jax.experimental import pallas as pl
from jax.experimental.pallas import tpu as pltpu
from jax.sharding import PartitionSpec as P

MESH = pl.DeviceIdType.MESH
REACH = 4
LANES = 128
F32 = jnp.float32


def kernel(tau_ref, lam_ref, out_ref, blk, lt, part, r1, s1, r2, xs, xr, fin,
           in_sem, zs, zr, xss, xrs, d1s, d1r, d2s, d2r, as_, ar, bs, br, hs, hr):
    depth = tau_ref.shape[0]
    pieces = tau_ref.shape[1] // LANES
    units = 2 * pieces
    rows = out_ref.shape[1]
    n_vir, n_occ = lax.axis_size("vir"), lax.axis_size("occ")
    n_y = n_occ // 2
    v, o = lax.axis_index("vir"), lax.axis_index("occ")
    core, x_lo = lax.rem(v, 2), lax.rem(lax.div(v, 2), 2)
    y, h = lax.div(o, 2), lax.rem(o, 2)
    y_up, y_dn, y_far = lax.rem(y + 1, n_y), lax.rem(y + n_y - 1, n_y), lax.rem(y + 2, n_y)
    z_dn = (lax.rem(v + n_vir - 4, n_vir), o)
    z_up = (lax.rem(v + 4, n_vir), o)
    x_nb = (v + 2 - 4 * x_lo, o)
    mate = (v + 1 - 2 * core, o)
    up, dn = (v, 2 * y_up + h), (v, 2 * y_dn + h)
    far = (v, o + 1 - 2 * h)

    def remote(src, dst, send, recv, to):
        return pltpu.make_async_remote_copy(
            src_ref=src, dst_ref=dst, send_sem=send, recv_sem=recv, device_id=to, device_id_type=MESH)

    def at(slot, p, s):
        return blk.at[slot, p, pl.ds(s * depth, depth)]

    def load(p, s):
        src = (tau_ref, lam_ref)[s]
        return pltpu.make_async_copy(src.at[:, pl.ds(p * LANES, LANES)], at(0, p, s), in_sem.at[2 * p + s])

    def z_copy(p, s):
        u = 2 * p + s
        return remote(at(0, p, s), at(4, p, s), zs.at[u], zr.at[u], z_dn)

    def x_copy(p, s):
        u = 2 * p + s
        return remote(at(4 - 4 * x_lo, p, s), at(2, p, s), xss.at[u], xrs.at[u], x_nb)

    def d1_copy(p, s):
        u = 2 * p + s
        return remote(at(2 - 2 * core, p, s), at(1, p, s), d1s.at[u], d1r.at[u], mate)

    def d2_copy(p, s):
        u = 2 * p + s
        return remote(at(4 - 2 * core, p, s), at(3, p, s), d2s.at[u], d2r.at[u], mate)

    def a_copy(t, j):
        src, dst, to = (
            (part.at[t, y_far, 0], r1.at[t, 0], up),
            (part.at[t, y_far, 1], r1.at[t, 1], dn),
            (part.at[t, y_up, 1], r2.at[t, 0, 1], up),
            (part.at[t, y_dn, 0], r2.at[t, 1, 0], dn),
        )[j]
        return remote(src, dst, as_.at[t, j], ar.at[t, j], to)

    def b_copy(t, j):
        return remote(s1.at[t, j], r2.at[t, j, j], bs.at[t, j], br.at[t, j], (up, dn)[j])

    def h_copy(t):
        return remote(xs.at[t], xr.at[t], hs.at[t], hr.at[t], far)

    def unit(t, i, k, p):
        acc = 0.5 * jnp.dot(lt[...], blk[k, p], preferred_element_type=F32)
        acc = acc.astype(jnp.bfloat16)
        for g in range(n_occ):
            part[t, g // 2, g % 2, i] = acc[g * rows:(g + 1) * rows]

    def send_parts(t):
        for j in range(4):
            a_copy(t, j).start()

    def pass_on(t):
        for j, near in ((0, y_up), (1, y_dn)):
            a_copy(t, j).wait_recv()
            s1[t, j] = (r1[t, j].astype(F32) + part[t, near, j].astype(F32)).astype(jnp.bfloat16)
            b_copy(t, j).start()

    def gather(t):
        for j in range(2):
            a_copy(t, 2 + j).wait_recv()
            b_copy(t, j).wait_recv()

        def total(g):
            return part[t, y, g].astype(F32) + r2[t, 0, g].astype(F32) + r2[t, 1, g].astype(F32)

        xs[t] = total(1 - h).astype(jnp.bfloat16)
        h_copy(t).start()
        fin[t] = total(h)

    for p in range(pieces):
        for s in range(2):
            load(p, s).start()

    barrier = pltpu.get_barrier_semaphore()
    for peer in (z_dn, z_up, x_nb, mate, up, dn, far):
        pl.semaphore_signal(barrier, inc=1, device_id=peer, device_id_type=MESH)
    pl.semaphore_wait(barrier, 7)

    for p in range(pieces):
        for s in range(2):
            load(p, s).wait()
            z_copy(p, s).start()

            @pl.when(x_lo == 1)
            def _():
                x_copy(p, s).start()

            @pl.when(core == 1)
            def _():
                d1_copy(p, s).start()

    for p in range(pieces):
        for s in range(2):
            lt[p * LANES:(p + 1) * LANES, (1 - s) * depth:(2 - s) * depth] = blk[0, p, s * depth:(s + 1) * depth].T

    for p in range(pieces):
        unit(0, p, 0, p)
    send_parts(0)

    def step(p, carry):
        t = p + 1
        for s in range(2):
            z_copy(p, s).wait_recv()

            @pl.when(x_lo == 0)
            def _():
                x_copy(p, s).start()

            @pl.when(core == 0)
            def _():
                d2_copy(p, s).start()

            x_copy(p, s).wait_recv()

            @pl.when(core == 0)
            def _():
                d1_copy(p, s).start()

            @pl.when(core == 1)
            def _():
                d2_copy(p, s).start()

            if s == 0:
                pass_on(t - 1)
        unit(t, 3, 4, p)
        unit(t, 1, 2, p)
        for s in range(2):
            d1_copy(p, s).wait_recv()
            d2_copy(p, s).wait_recv()
        unit(t, 0, 1, p)
        unit(t, 2, 3, p)
        send_parts(t)

        @pl.when(p > 0)
        def _():
            gather(t - 2)

        return carry

    lax.fori_loop(0, pieces, step, 0)
    pass_on(pieces)
    gather(pieces - 1)
    gather(pieces)

    for t in range(pieces + 1):
        h_copy(t).wait_recv()
        for i in range(4):
            k, p = (0, i) if t == 0 else (1 + i, t - 1)
            out_ref[k, :, p * LANES:(p + 1) * LANES] = fin[t, i] + xr[t, i].astype(F32)

    for p in range(pieces):
        for s in range(2):
            for copy in (z_copy(p, s), x_copy(p, s), d1_copy(p, s), d2_copy(p, s)):
                copy.wait_send()
    for t in range(pieces + 1):
        for j in range(4):
            a_copy(t, j).wait_send()
        for j in range(2):
            b_copy(t, j).wait_send()
        h_copy(t).wait_send()


def on_device(tau_amps, lambda_amps):
    depth, cols = tau_amps.shape
    pieces, n_occ = cols // LANES, lax.axis_size("occ")
    rows, batches, units = cols // n_occ, cols // LANES + 1, 2 * (cols // LANES)
    bf16, dma = jnp.bfloat16, pltpu.SemaphoreType.DMA
    chunk = (4, rows, LANES)
    out = pl.pallas_call(
        kernel,
        out_shape=jax.ShapeDtypeStruct((REACH + 1, rows, cols), F32),
        in_specs=[pl.BlockSpec(memory_space=pl.ANY)] * 2,
        out_specs=pl.BlockSpec(memory_space=pltpu.VMEM),
        scratch_shapes=[
            pltpu.VMEM((5, pieces, 2 * depth, LANES), bf16),
            pltpu.VMEM((cols, 2 * depth), bf16),
            pltpu.VMEM((batches, n_occ // 2, 2, *chunk), bf16),
            pltpu.VMEM((batches, 2, *chunk), bf16),
            pltpu.VMEM((batches, 2, *chunk), bf16),
            pltpu.VMEM((batches, 2, 2, *chunk), bf16),
            pltpu.VMEM((batches, *chunk), bf16),
            pltpu.VMEM((batches, *chunk), bf16),
            pltpu.VMEM((batches, *chunk), F32),
            *[dma((units,))] * 9,
            dma((batches, 4)), dma((batches, 4)),
            dma((batches, 2)), dma((batches, 2)),
            dma((batches,)), dma((batches,)),
        ],
        compiler_params=pltpu.CompilerParams(collective_id=0, has_side_effects=True),
    )(tau_amps, lambda_amps)
    return jnp.transpose(out, (1, 0, 2))


def solution(mesh):
    placed = (P("occ", "vir"), P("occ", "vir"))
    return jax.shard_map(
        on_device,
        mesh=mesh,
        in_specs=placed,
        out_specs=P(("vir", "occ"), None, None),
        check_vma=False,
    )
```

time: 116 us -> 62.5 us (0.54)
  the two profiles are of different devices: /device:TPU:8 before, /device:TPU:2 now
where the time goes in v1:
time: 62.5 us; the launch traced here: 62.3 us
  Pallas kernels  60.3 us (96%)
  local copies, waits for them, and re-layouts  1.99 us (3%)
    pallas_call x1, Pallas kernels, on_device(): pl.pallas_call(kernel, out_shape=jax.ShapeDtypeStruct((REACH + 1, rows, c...  60.3 us
    unnamed x1, local copies, waits for them, and re-layouts  1.99 us

profile of v1, /device:TPU:2, one launch (start us, length us, event | category | flops | bytes accessed | tf_op | source)
XLA Modules:
  0.0 62.3 jit_solution(14561429301770470372)
XLA Ops:
  0.0 60.3 %shard_map.28 = f32[5,64,512]{2,1,0:T(8,128)} custom-call(bf16[512,512]{1,0:T(8,128)(2,1)} %tau_ref.1, bf16[512,512]{1,0:T(8,128)(2,1)} %lam_ref.1), custom_call_target="tpu_custom_call" | custom-call | tf_op jit(solution)/shard_map/pallas_call | solution.py:202
  60.3 2.0 %copy.4 = f32[64,5,512]{2,0,1:T(8,128)} copy(f32[64,5,512]{2,0,1:T(8,128)} %bitcast.1) | data formatting | bytes 1310720

commit v2 on v1

--- a/solution.py
+++ b/solution.py
@@ -12,7 +12,7 @@
 
 
 def kernel(tau_ref, lam_ref, out_ref, blk, lt, part, r1, s1, r2, xs, xr, fin,
-           in_sem, zs, zr, xss, xrs, d1s, d1r, d2s, d2r, as_, ar, bs, br, hs, hr):
+           in_sem, zs, zr, xss, xrs, d1s, d1r, d2s, d2r, as_, ar, bs, br, hs, hr, go):
     depth = tau_ref.shape[0]
     pieces = tau_ref.shape[1] // LANES
     units = 2 * pieces
@@ -20,6 +20,7 @@
     n_vir, n_occ = lax.axis_size("vir"), lax.axis_size("occ")
     n_y = n_occ // 2
     v, o = lax.axis_index("vir"), lax.axis_index("occ")
+    z = lax.div(v, 4)
     core, x_lo = lax.rem(v, 2), lax.rem(lax.div(v, 2), 2)
     y, h = lax.div(o, 2), lax.rem(o, 2)
     y_up, y_dn, y_far = lax.rem(y + 1, n_y), lax.rem(y + n_y - 1, n_y), lax.rem(y + 2, n_y)
@@ -105,14 +106,21 @@
             load(p, s).start()
 
     barrier = pltpu.get_barrier_semaphore()
-    for peer in (z_dn, z_up, x_nb, mate, up, dn, far):
+    for peer in (z_dn, x_nb, mate, up, dn, far):
         pl.semaphore_signal(barrier, inc=1, device_id=peer, device_id_type=MESH)
-    pl.semaphore_wait(barrier, 7)
+    pl.semaphore_wait(barrier, 6)
+    pl.semaphore_signal(go, inc=1, device_id=z_up, device_id_type=MESH)
+
+    def z_send():
+        pl.semaphore_wait(go, 1)
+        for p in range(pieces):
+            for s in range(2):
+                z_copy(p, s).start()
+
 
     for p in range(pieces):
         for s in range(2):
             load(p, s).wait()
-            z_copy(p, s).start()
 
             @pl.when(x_lo == 1)
             def _():
@@ -122,16 +130,21 @@
             def _():
                 d1_copy(p, s).start()
 
+    @pl.when(z > 0)
+    def _():
+        z_send()
+
     for p in range(pieces):
         for s in range(2):
             lt[p * LANES:(p + 1) * LANES, (1 - s) * depth:(2 - s) * depth] = blk[0, p, s * depth:(s + 1) * depth].T
 
-    for p in range(pieces):
-        unit(0, p, 0, p)
-    send_parts(0)
+    for t in range(2):
+        for i in range(2):
+            unit(t, i, 0, 2 * t + i)
+        send_parts(t)
+    pass_on(0)
 
     def step(p, carry):
-        t = p + 1
         for s in range(2):
             z_copy(p, s).wait_recv()
 
@@ -154,38 +167,42 @@
                 d2_copy(p, s).start()
 
             if s == 0:
-                pass_on(t - 1)
-        unit(t, 3, 4, p)
-        unit(t, 1, 2, p)
+                pass_on(2 * p + 1)
+
+        @pl.when((p == 0) & (z == 0))
+        def _():
+            z_send()
+
+        unit(2 * p + 2, 0, 4, p)
+        unit(2 * p + 2, 1, 2, p)
+        send_parts(2 * p + 2)
+        gather(2 * p)
         for s in range(2):
             d1_copy(p, s).wait_recv()
             d2_copy(p, s).wait_recv()
-        unit(t, 0, 1, p)
-        unit(t, 2, 3, p)
-        send_parts(t)
-
-        @pl.when(p > 0)
-        def _():
-            gather(t - 2)
-
+        unit(2 * p + 3, 0, 1, p)
+        unit(2 * p + 3, 1, 3, p)
+        send_parts(2 * p + 3)
+        pass_on(2 * p + 2)
+        gather(2 * p + 1)
         return carry
 
     lax.fori_loop(0, pieces, step, 0)
-    pass_on(pieces)
-    gather(pieces - 1)
-    gather(pieces)
-
-    for t in range(pieces + 1):
+    pass_on(2 * pieces + 1)
+    gather(2 * pieces)
+    gather(2 * pieces + 1)
+
+    for t in range(2 * pieces + 2):
         h_copy(t).wait_recv()
-        for i in range(4):
-            k, p = (0, i) if t == 0 else (1 + i, t - 1)
+        for i in range(2):
+            k, p = (0, 2 * t + i) if t < 2 else (((4, 2), (1, 3))[t % 2][i], t // 2 - 1)
             out_ref[k, :, p * LANES:(p + 1) * LANES] = fin[t, i] + xr[t, i].astype(F32)
 
     for p in range(pieces):
         for s in range(2):
             for copy in (z_copy(p, s), x_copy(p, s), d1_copy(p, s), d2_copy(p, s)):
                 copy.wait_send()
-    for t in range(pieces + 1):
+    for t in range(2 * pieces + 2):
         for j in range(4):
             a_copy(t, j).wait_send()
         for j in range(2):
@@ -196,12 +213,12 @@
 def on_device(tau_amps, lambda_amps):
     depth, cols = tau_amps.shape
     pieces, n_occ = cols // LANES, lax.axis_size("occ")
-    rows, batches, units = cols // n_occ, cols // LANES + 1, 2 * (cols // LANES)
+    rows, batches, units = cols // n_occ, 2 * (cols // LANES) + 2, 2 * (cols // LANES)
     bf16, dma = jnp.bfloat16, pltpu.SemaphoreType.DMA
-    chunk = (4, rows, LANES)
+    chunk = (2, rows, LANES)
     out = pl.pallas_call(
         kernel,
-        out_shape=jax.ShapeDtypeStruct((REACH + 1, rows, cols), F32),
+        out_shape=pltpu.VMEM((REACH + 1, rows, cols), F32),
         in_specs=[pl.BlockSpec(memory_space=pl.ANY)] * 2,
         out_specs=pl.BlockSpec(memory_space=pltpu.VMEM),
         scratch_shapes=[
@@ -218,6 +235,7 @@
             dma((batches, 4)), dma((batches, 4)),
             dma((batches, 2)), dma((batches, 2)),
             dma((batches,)), dma((batches,)),
+            pltpu.SemaphoreType.REGULAR,
         ],
         compiler_params=pltpu.CompilerParams(collective_id=0, has_side_effects=True),
     )(tau_amps, lambda_amps)

time: 62.5 us -> 58 us (0.928)
  the two profiles are of different devices: /device:TPU:2 before, /device:TPU:486 now
where the time goes in v2:
time: 58 us; the launch traced here: 57.8 us
  Pallas kernels  57 us (98%)
  local copies, waits for them, and re-layouts  0.84 us (1%)
    pallas_call x1, Pallas kernels, on_device(): pl.pallas_call(kernel, out_shape=pltpu.VMEM((REACH + 1, rows, cols), F32)...  57 us

profile of v2, /device:TPU:486, one launch (start us, length us, event | category | flops | bytes accessed | tf_op | source)
XLA Modules:
  0.0 57.8 jit_solution(2207465506392953689)
XLA Ops:
  0.0 57.0 %shard_map.28 = f32[5,64,512]{2,1,0:T(8,128)S(1)} custom-call(bf16[512,512]{1,0:T(8,128)(2,1)} %tau_ref.1, bf16[512,512]{1,0:T(8,128)(2,1)} %lam_ref.1), custom_call_target="tpu_custom_call" | custom-call | tf_op jit(solution)/shard_map/pallas_call | solution.py:219
  57.0 0.8 %copy.4 = f32[64,5,512]{2,0,1:T(8,128)} copy(f32[64,5,512]{2,0,1:T(8,128)S(1)} %bitcast.1) | data formatting | bytes 1310720
